TPU v7x, 32 devices: a whole 2x2x4 slice. The times are simulated.
32 devices in a mesh: dp: 8 (over y, x, core), mp: 4 (over z).
Axes of the slice: x: 2, y: 2, z: 4, core: 2. Of those that a mesh axis runs over, the one named last changes fastest.
Arguments:
- hidden: bfloat16 [8192, 2048], P('dp'), may hold values from -6 to 6
- cotangent: bfloat16 [8192, 2048], P('dp'), may hold values from -6 to 6
- lengths: int32 [16], P('dp'), may hold values from 64 to 512, as said below
- input_gain: bfloat16 [2048], P('dp'), may hold values from 0.5 to 1.5
- input_shift: bfloat16 [2048], P('dp'), may hold values from -1.25 to 1.25
- triple_weight: bfloat16 [2048, 3, 2048], P('dp', None, 'mp'), may hold values from -0.125 to 0.125
- triple_bias: bfloat16 [2, 2048], P(None, 'mp'), may hold values from -1.25 to 1.25
- merge_weight: bfloat16 [2048, 2048], P('mp', 'dp'), may hold values from -0.5 to 0.5
- merge_bias: bfloat16 [2048], P('dp'), may hold values from -1.25 to 1.25
- middle_gain: bfloat16 [2048], P('dp'), may hold values from 0.5 to 1.5
- middle_shift: bfloat16 [2048], P('dp'), may hold values from -1.25 to 1.25
- expand_weight: bfloat16 [2048, 8192], P('dp', 'mp'), may hold values from -0.125 to 0.125
- expand_bias: bfloat16 [8192], P('mp'), may hold values from -1.25 to 1.25
- reduce_weight: bfloat16 [8192, 2048], P('mp', 'dp'), may hold values from -0.0625 to 0.0625
- reduce_bias: bfloat16 [2048], P('dp'), may hold values from -1.25 to 1.25
Outputs:
- layer_output: bfloat16 [8192, 2048], P('dp')
- hidden_grad: bfloat16 [8192, 2048], P('dp')
- input_gain_grad: float32 [2048], P('dp')
- input_shift_grad: float32 [2048], P('dp')
- triple_weight_grad: float32 [2048, 3, 2048], P('dp', None, 'mp')
- triple_bias_grad: float32 [2, 2048], P(None, 'mp')
- merge_weight_grad: float32 [2048, 2048], P('mp', 'dp')
- merge_bias_grad: float32 [2048], P('dp')
- middle_gain_grad: float32 [2048], P('dp')
- middle_shift_grad: float32 [2048], P('dp')
- expand_weight_grad: float32 [2048, 8192], P('dp', 'mp')
- expand_bias_grad: float32 [8192], P('mp')
- reduce_weight_grad: float32 [8192, 2048], P('mp', 'dp')
- reduce_bias_grad: float32 [2048], P('dp')
- branch_rms: float32 [3], replicated
Inputs may be any that keep to these rules, and one draw needn't show every extreme that they name: `lengths`: each slot's valid tokens stand at its start; in every draw some slot is full (512 valid tokens).
All inputs are finite; a program needn't handle non-finite values.
Results may differ from a plain program's by a relative error of at most 0.023.
Values may be sent and summed in bfloat16 or wider, within the bound.
A program may use at most 256 MiB of HBM per device.

v0:
```python
import jax
import jax.numpy as jnp
from jax import lax
from jax.sharding import PartitionSpec as P

HEADS = 32
HEAD_DIM = 64
SLOT = 512
MICRO = 2


def layer_norm(values, gain_vec, shift_vec):
    center = values - jnp.mean(values, axis=-1, keepdims=True)
    spread = jnp.mean(center * center, axis=-1, keepdims=True)
    return center * lax.rsqrt(spread + 1e-05) * gain_vec + shift_vec


def gelu_exact(values):
    return jax.nn.gelu(values, approximate=False)


def attention_scores(query_low, key_low, slopes, length):
    raw_scores = jnp.einsum("qhe,khe->hqk", query_low, key_low, preferred_element_type=jnp.float32)
    places = jnp.arange(query_low.shape[0], dtype=jnp.int32)
    key_place = places.astype(jnp.float32)
    scores = (raw_scores + slopes[:, None, None] * key_place[None, None, :]) * 0.125
    allowed = (places[None, :] <= places[:, None]) & (places[None, :] < length)
    return jnp.where(allowed[None], scores, -1000000000.0)


def local(
    hidden,
    cotangent,
    lengths,
    input_gain,
    input_shift,
    triple_weight,
    triple_bias,
    merge_weight,
    merge_bias,
    middle_gain,
    middle_shift,
    expand_weight,
    expand_bias,
    reduce_weight,
    reduce_bias,
):
    slot = SLOT
    width = hidden.shape[1]
    head_cols = triple_weight.shape[2]
    unit_cols = expand_weight.shape[1]
    local_heads = head_cols // HEAD_DIM
    head_start = lax.axis_index("mp") * local_heads
    slopes = 2.0 ** (
        -8.0
        * (head_start + jnp.arange(local_heads, dtype=jnp.int32) + 1).astype(jnp.float32)
        / HEADS
    )
    bias_pair = triple_bias.astype(jnp.float32)
    unit_shift = expand_bias.astype(jnp.float32)
    attention_kept = (
        lax.all_gather(input_gain, "dp", axis=0, tiled=True),
        lax.all_gather(input_shift, "dp", axis=0, tiled=True),
        lax.all_gather(triple_weight, "dp", axis=0, tiled=True),
        lax.all_gather(merge_weight, "dp", axis=1, tiled=True),
        lax.all_gather(merge_bias, "dp", axis=0, tiled=True),
    )
    feed_kept = (
        lax.all_gather(middle_gain, "dp", axis=0, tiled=True),
        lax.all_gather(middle_shift, "dp", axis=0, tiled=True),
        lax.all_gather(expand_weight, "dp", axis=0, tiled=True),
        lax.all_gather(reduce_weight, "dp", axis=1, tiled=True),
        lax.all_gather(reduce_bias, "dp", axis=0, tiled=True),
    )
    acc_triple = jnp.zeros((width, 3, head_cols), jnp.float32)
    acc_merge = jnp.zeros((head_cols, width), jnp.float32)
    acc_expand = jnp.zeros((width, unit_cols), jnp.float32)
    acc_reduce = jnp.zeros((unit_cols, width), jnp.float32)
    acc_gain_one = jnp.zeros((width,), jnp.float32)
    acc_shift_one = jnp.zeros((width,), jnp.float32)
    acc_merge_bias = jnp.zeros((width,), jnp.float32)
    acc_gain_two = jnp.zeros((width,), jnp.float32)
    acc_shift_two = jnp.zeros((width,), jnp.float32)
    acc_reduce_bias = jnp.zeros((width,), jnp.float32)
    acc_pair_bias = jnp.zeros((2, head_cols), jnp.float32)
    acc_unit_bias = jnp.zeros((unit_cols,), jnp.float32)
    square_sums = jnp.zeros((4,), jnp.float32)
    output_parts = []
    grad_parts = []
    for batch_index in range(MICRO):
        start = batch_index * slot
        token_rows = hidden[start : start + slot].astype(jnp.float32)
        length = lengths[batch_index]
        valid_rows = (jnp.arange(slot, dtype=jnp.int32) < length)[:, None]
        gain_one, shift_one, triple_full, merge_full, merge_shift = attention_kept
        gain_two, shift_two, expand_full, reduce_full, reduce_shift = feed_kept
        gain_one = gain_one.astype(jnp.float32)
        shift_one = shift_one.astype(jnp.float32)
        gain_two = gain_two.astype(jnp.float32)
        shift_two = shift_two.astype(jnp.float32)
        norm_in = layer_norm(token_rows, gain_one, shift_one).astype(jnp.bfloat16)
        triple = jnp.einsum("td,dcf->tcf", norm_in, triple_full, preferred_element_type=jnp.float32)
        query_low = (
            (triple[:, 0] + bias_pair[0]).astype(jnp.bfloat16).reshape(slot, local_heads, HEAD_DIM)
        )
        key_low = triple[:, 1].astype(jnp.bfloat16).reshape(slot, local_heads, HEAD_DIM)
        value_low = (
            (triple[:, 2] + bias_pair[1]).astype(jnp.bfloat16).reshape(slot, local_heads, HEAD_DIM)
        )
        scores = attention_scores(query_low, key_low, slopes, length)
        log_total = jax.nn.logsumexp(scores, axis=-1)
        attention_weights = jnp.exp(scores - log_total[..., None]).astype(jnp.bfloat16)
        mixed_heads = jnp.einsum(
            "hqk,khe->qhe", attention_weights, value_low, preferred_element_type=jnp.float32
        )
        mixed_heads = mixed_heads.reshape(slot, head_cols).astype(jnp.bfloat16)
        attention_part = jnp.dot(mixed_heads, merge_full, preferred_element_type=jnp.float32)
        attention_branch = lax.psum(attention_part.astype(jnp.bfloat16), "mp").astype(
            jnp.float32
        ) + merge_shift.astype(jnp.float32)
        residual = token_rows + attention_branch
        norm_mid = layer_norm(residual, gain_two, shift_two).astype(jnp.bfloat16)
        token_count = length.astype(jnp.float32)
        expand_pre = jnp.dot(norm_mid, expand_full, preferred_element_type=jnp.float32) + unit_shift
        activation = gelu_exact(expand_pre).astype(jnp.bfloat16)
        feed_part = jnp.dot(activation, reduce_full, preferred_element_type=jnp.float32)
        feed_branch = lax.psum(feed_part.astype(jnp.bfloat16), "mp").astype(
            jnp.float32
        ) + reduce_shift.astype(jnp.float32)
        result = residual + feed_branch
        output_parts.append(jnp.where(valid_rows, result, 0.0).astype(jnp.bfloat16))
        square_sums = square_sums + jnp.stack(
            [
                jnp.sum(jnp.where(valid_rows, result * result, 0.0)),
                jnp.sum(jnp.where(valid_rows, attention_branch * attention_branch, 0.0)),
                jnp.sum(jnp.where(valid_rows, feed_branch * feed_branch, 0.0)),
                token_count,
            ]
        )
        grad_out = jnp.where(valid_rows, cotangent[start : start + slot].astype(jnp.float32), 0.0)
        grad_feed = grad_out.astype(jnp.bfloat16)
        acc_reduce_bias = acc_reduce_bias + jnp.sum(grad_out, axis=0)
        acc_reduce = acc_reduce + jnp.dot(
            activation.T, grad_feed, preferred_element_type=jnp.float32
        )
        grad_act = jnp.dot(grad_feed, reduce_full.T, preferred_element_type=jnp.float32)
        gelu_value, gelu_back = jax.vjp(gelu_exact, expand_pre)
        grad_pre = gelu_back(grad_act)[0].astype(jnp.bfloat16)
        acc_unit_bias = acc_unit_bias + jnp.sum(grad_pre, axis=0, dtype=jnp.float32)
        acc_expand = acc_expand + jnp.dot(norm_mid.T, grad_pre, preferred_element_type=jnp.float32)
        mid_part = jnp.dot(grad_pre, expand_full.T, preferred_element_type=jnp.float32)
        grad_mid = lax.psum(mid_part.astype(jnp.bfloat16), "mp").astype(jnp.float32)
        norm_value, norm_back = jax.vjp(layer_norm, residual, gain_two, shift_two)
        grad_resid_norm, grad_gain_two, grad_shift_two = norm_back(grad_mid)
        acc_gain_two = acc_gain_two + grad_gain_two
        acc_shift_two = acc_shift_two + grad_shift_two
        grad_residual = grad_out + grad_resid_norm
        grad_branch = grad_residual.astype(jnp.bfloat16)
        acc_merge_bias = acc_merge_bias + jnp.sum(grad_branch, axis=0, dtype=jnp.float32)
        acc_merge = acc_merge + jnp.dot(
            mixed_heads.T, grad_branch, preferred_element_type=jnp.float32
        )
        grad_mixed = jnp.dot(grad_branch, merge_full.T, preferred_element_type=jnp.float32)
        grad_mixed = grad_mixed.astype(jnp.bfloat16).reshape(slot, local_heads, HEAD_DIM)
        again_scores = attention_scores(query_low, key_low, slopes, length)
        soft_weights = jnp.exp(again_scores - log_total[..., None])
        grad_probs = jnp.einsum(
            "qhe,khe->hqk", grad_mixed, value_low, preferred_element_type=jnp.float32
        )
        grad_value = jnp.einsum(
            "hqk,qhe->khe",
            soft_weights.astype(jnp.bfloat16),
            grad_mixed,
            preferred_element_type=jnp.float32,
        ).astype(jnp.bfloat16)
        row_terms = jnp.sum(soft_weights * grad_probs, axis=-1, keepdims=True)
        grad_scores = (soft_weights * (grad_probs - row_terms)).astype(jnp.bfloat16)
        grad_query = (
            0.125
            * jnp.einsum("hqk,khe->qhe", grad_scores, key_low, preferred_element_type=jnp.float32)
        ).astype(jnp.bfloat16)
        grad_key = (
            0.125
            * jnp.einsum("hqk,qhe->khe", grad_scores, query_low, preferred_element_type=jnp.float32)
        ).astype(jnp.bfloat16)
        grad_triple = jnp.stack([grad_query, grad_key, grad_value], axis=1).reshape(
            slot, 3, head_cols
        )
        acc_pair_bias = acc_pair_bias + jnp.stack(
            [
                jnp.sum(grad_triple[:, 0], axis=0, dtype=jnp.float32),
                jnp.sum(grad_triple[:, 2], axis=0, dtype=jnp.float32),
            ]
        )
        acc_triple = acc_triple + jnp.einsum(
            "td,tcf->dcf", norm_in, grad_triple, preferred_element_type=jnp.float32
        )
        grad_in_part = jnp.einsum(
            "tcf,dcf->td", grad_triple, triple_full, preferred_element_type=jnp.float32
        )
        grad_in = lax.psum(grad_in_part.astype(jnp.bfloat16), "mp").astype(jnp.float32)
        first_value, first_back = jax.vjp(layer_norm, token_rows, gain_one, shift_one)
        grad_rows_norm, grad_gain_one, grad_shift_one = first_back(grad_in)
        acc_gain_one = acc_gain_one + grad_gain_one
        acc_shift_one = acc_shift_one + grad_shift_one
        input_rows_grad = (grad_residual + grad_rows_norm).astype(jnp.bfloat16)
        grad_parts.append(input_rows_grad)
    owned = (
        lax.psum_scatter(
            acc_triple.astype(jnp.bfloat16), "dp", scatter_dimension=0, tiled=True
        ).astype(jnp.float32),
        lax.psum_scatter(
            acc_merge.astype(jnp.bfloat16), "dp", scatter_dimension=1, tiled=True
        ).astype(jnp.float32),
        lax.psum_scatter(
            acc_expand.astype(jnp.bfloat16), "dp", scatter_dimension=0, tiled=True
        ).astype(jnp.float32),
        lax.psum_scatter(
            acc_reduce.astype(jnp.bfloat16), "dp", scatter_dimension=1, tiled=True
        ).astype(jnp.float32),
        lax.psum_scatter(
            acc_gain_one.astype(jnp.bfloat16), "dp", scatter_dimension=0, tiled=True
        ).astype(jnp.float32),
        lax.psum_scatter(
            acc_shift_one.astype(jnp.bfloat16), "dp", scatter_dimension=0, tiled=True
        ).astype(jnp.float32),
        lax.psum_scatter(
            acc_merge_bias.astype(jnp.bfloat16), "dp", scatter_dimension=0, tiled=True
        ).astype(jnp.float32),
        lax.psum_scatter(
            acc_gain_two.astype(jnp.bfloat16), "dp", scatter_dimension=0, tiled=True
        ).astype(jnp.float32),
        lax.psum_scatter(
            acc_shift_two.astype(jnp.bfloat16), "dp", scatter_dimension=0, tiled=True
        ).astype(jnp.float32),
        lax.psum_scatter(
            acc_reduce_bias.astype(jnp.bfloat16), "dp", scatter_dimension=0, tiled=True
        ).astype(jnp.float32),
    )
    pair_grad, unit_grad, total_sums = lax.psum((acc_pair_bias, acc_unit_bias, square_sums), "dp")
    root_means = jnp.sqrt(total_sums[:3] / (total_sums[3] * width))
    layer_output = jnp.concatenate(output_parts, axis=0)
    hidden_grad = jnp.concatenate(grad_parts, axis=0)
    return (
        layer_output,
        hidden_grad,
        owned[4],
        owned[5],
        owned[0],
        pair_grad,
        owned[1],
        owned[6],
        owned[7],
        owned[8],
        owned[2],
        unit_grad,
        owned[3],
        owned[9],
        root_means,
    )


def solution(mesh):
    return jax.shard_map(
        local,
        mesh=mesh,
        in_specs=(
            P("dp", None),
            P("dp", None),
            P("dp"),
            P("dp"),
            P("dp"),
            P("dp", None, "mp"),
            P(None, "mp"),
            P("mp", "dp"),
            P("dp"),
            P("dp"),
            P("dp"),
            P("dp", "mp"),
            P("mp"),
            P("mp", "dp"),
            P("dp"),
        ),
        out_specs=(
            P("dp", None),
            P("dp", None),
            P("dp"),
            P("dp"),
            P("dp", None, "mp"),
            P(None, "mp"),
            P("mp", "dp"),
            P("dp"),
            P("dp"),
            P("dp"),
            P("dp", "mp"),
            P("mp"),
            P("mp", "dp"),
            P("dp"),
            P(),
        ),
        check_vma=False,
    )
```

profile of v0, /device:TPU:0, one launch (start us, length us, event | category | flops | bytes accessed | tf_op | source)
XLA Modules:
  0.0 1231.0 jit_solution(12049603003931523445)
XLA Ops:
  17.5 10.6 all-gather
  37.4 22.4 %all-gather.11.cloned.1.call-done = bf16[2048,3,512]{0,2,1:T(8,128)(2,1)} async-done(((bf16[256,3,512]{0,2,1:T(8,128)(2,1)}), bf16[2048,3,512]{0,2,1:T(8,128)(2,1)}) %all-gather.11.cloned.1.call-update) | async-done | bytes 6291472 | tf_op jit(solution)/shard_map/all_gather | solution.py:64
  73.6 16.2 %all-gather.13.cloned.1.call-done = bf16[512,2048]{1,0:T(8,128)(2,1)} async-done(((bf16[512,256]{1,0:T(8,128)(2,1)}), bf16[512,2048]{1,0:T(8,128)(2,1)}) %all-gather.13.cloned.1.call-update) | async-done | bytes 2097168 | tf_op jit(solution)/shard_map/all_gather | solution.py:65
  104.3 76.0 %all-reduce.15.cloned.1.call-done = bf16[512,2048]{1,0:T(8,128)(2,1)} async-done(((bf16[512,2048]{1,0:T(8,128)(2,1)}), bf16[512,2048]{1,0:T(8,128)(2,1)}) %all-reduce.15.cloned.1.call-update) | async-done | bytes 2097168 | tf_op jit(solution)/shard_map/psum | solution.py:118
  221.1 66.0 %all-reduce.17.cloned.1.call-done = bf16[512,2048]{1,0:T(8,128)(2,1)} async-done(((bf16[512,2048]{1,0:T(8,128)(2,1)}), bf16[512,2048]{1,0:T(8,128)(2,1)}) %all-reduce.17.cloned.1.call-update) | async-done | bytes 2097168 | tf_op jit(solution)/shard_map/psum | solution.py:118
  293.0 49.2 %all-gather.15.cloned.1.call-done = bf16[2048,2048]{1,0:T(8,128)(2,1)} async-done(((bf16[256,2048]{1,0:T(8,128)(2,1)}), bf16[2048,2048]{1,0:T(8,128)(2,1)}) %all-gather.15.cloned.1.call-update) | async-done | bytes 8388624 | tf_op jit(solution)/shard_map/all_gather | solution.py:71
  353.0 26.4 %multiply_convert_fusion.3 = (bf16[512,2048]{1,0:T(8,128)(2,1)}, f32[512,2048]{1,0:T(8,128)}, bf16[512,2048]{1,0:T(8,128)(2,1)}, f32[512,2048]{1,0:T(8,128)}, f32[512,2048]{1,0:T(8,128)}) fusion(f32[2048]{0:T(1024)S(1)} %convert_element_type.369, f32[512,2048]{1,0:T(8,128)S(1)} %fusion.108, bf16[2048,2048]{1,0:T(8,128)(2,1)S(1)} %copy-done.105, ...), kind=kOutput, calls=%fused_computation.120 | convolution fusion | flops 4442816512 | bytes 33591296 | tf_op jit(solution)/shard_map/dot_general | solution.py:124
  379.4 20.4 %all-gather.17.cloned.1.call-done = bf16[2048,2048]{1,0:T(8,128)(2,1)} async-done(((bf16[2048,256]{1,0:T(8,128)(2,1)}), bf16[2048,2048]{1,0:T(8,128)(2,1)}) %all-gather.17.cloned.1.call-update) | async-done | bytes 8388624 | tf_op jit(solution)/shard_map/all_gather | solution.py:72
  399.8 12.9 %convert_reduce_fusion.6 = (f32[2048]{0:T(1024)}, bf16[512,2048]{1,0:T(8,128)(2,1)S(1)}) fusion(f32[512,2048]{1,0:T(8,128)} %get-tuple-element.85, bf16[2048,2048]{1,0:T(8,128)(2,1)} %all-gather.17.cloned.1.call-done, pred[512]{0:T(512)(128)(4,1)S(1)} %iota_compare_fusion.1, bf16[1024,2048]{1,0:T(8,128)(2,1)} %param.16, f32[512,2048]{1,0:T(8,128)} %copy-done.120, ...), kind=kOutput, calls=%fused_computation.81 | convolution fusion | flops 4315936768 | bytes 20988416 | tf_op jit(solution)/shard_map/dot_general | solution.py:146
  412.7 9.9 convolution_convert_fusion
  422.6 11.5 convert_reduce_fusion.7
  434.1 10.0 convolution_convert_fusion.1
  468.9 281.5 %all-reduce.21.cloned.1.call-done = (bf16[512,2048]{1,0:T(8,128)(2,1)}, bf16[512,2048]{1,0:T(8,128)(2,1)}, bf16[512,2048]{1,0:T(8,128)(2,1)}, bf16[512,2048]{1,0:T(8,128)(2,1)}) async-done(((bf16[512,2048]{1,0:T(8,128)(2,1)}, bf16[512,2048]{1,0:T(8,128)(2,1)}, bf16[512,2048]{1,0:T(8,128)(2,1)}, bf16[512,2048]{1,0:T(8,128)(2,1)}), (bf16[512,2048]{1,0:T(8,128)(2,1)}, bf16[512,2048]{1,0:T(8,128)(2,1)}, ...) | async-done | bytes 8388624 | tf_op jit(solution)/shard_map/psum | solution.py:127
  750.5 14.7 %select_reduce_fusion.5 = (f32[]{:T(128)}, f32[512]{0:T(512)S(1)}, f32[512]{0:T(512)S(1)}, f32[]{:T(128)}, f32[]{:T(128)}, /*index=5*/f32[]{:T(128)}, f32[]{:T(1...) fusion(bf16[512,2048]{1,0:T(8,128)(2,1)} %get-tuple-element.67,, ...), kind=kLoop, calls=%fused_computation.80 | loop fusion | flops 55567360 | bytes 25224216 | tf_op jit(solution)/shard_map/reduce_sum | solution.py:134
  854.1 13.8 %fusion.106 = f32[2048,2048]{1,0:T(8,128)} fusion(bf16[512,2048]{1,0:T(8,128)(2,1)} %copy-done.119, f32[2048]{0:T(1024)S(1)} %bitcast.180, f32[2048]{0:T(1024)S(1)} %bitcast.161, f32[512]{0:T(512)S(1)} %copy-done.74, bf16[512,2048]{1,0:T(8,128)(2,1)} %all-reduce.15.cloned.1.call-done, f32[512]{0:T(512)S(1)} %broadcast_multiply_fusion.3, ...), kind=kOutput, calls=%fused_computation.249 | convolution fusion | flops 4304404480 | bytes 23097344 | tf_op jit(solution)/shard_map/dot_general | solution.py:150
  867.9 15.6 %add_convert_fusion.1 = bf16[2048,2048]{1,0:T(8,128)(2,1)} fusion(f32[2048,2048]{1,0:T(8,128)} %fusion.106, bf16[512,2048]{1,0:T(8,128)(2,1)} %copy-done.121, f32[512]{0:T(512)S(1)} %copy-done.72, f32[2048]{0:T(1024)S(1)} %bitcast.181, f32[2048]{0:T(1024)S(1)} %bitcast.162, bf16[512,2048]{1,0:T(8,128)(2,1)} %all-reduce.17.cloned.1.call-done, ...), kind=kOutput, calls=%fused_computation.1 | convolution fusion | flops 4312793088 | bytes 31485952 | tf_op jit(solution)/shard_map/dot_general | solution.py:150
  885.0 10.0 fusion.71
  895.0 11.0 add_convert_fusion
  931.9 25.5 %all-reduce.6 = (f32[2,512]{1,0:T(2,128)}, f32[2048]{0:T(1024)}, f32[4]{0:T(128)S(1)}) all-reduce(f32[2,512]{1,0:T(2,128)S(1)} %maximum_add_fusion, f32[2048]{0:T(1024)S(1)} %add.360, f32[4]{0:T(128)S(1)} %maximum_add_fusion.1), channel_id=1, replica_groups=mesh['dp'=8,'mp'=4] {'dp'}, use_global_device_ids=true, to_apply=%region_41.42 | all-reduce | flops 3076 | bytes 24608 | tf_op jit(solution)/shard_map/psum | solution.py:240
  965.2 42.5 %all-reduce.19.cloned.1.call-done = (bf16[512,2048]{1,0:T(8,128)(2,1)}, bf16[512,2048]{1,0:T(8,128)(2,1)}) async-done(((bf16[512,2048]{1,0:T(8,128)(2,1)}, bf16[512,2048]{1,0:T(8,128)(2,1)}), (bf16[512,2048]{1,0:T(8,128)(2,1)}, bf16[512,2048]{1,0:T(8,128)(2,1)})) %all-reduce.19.cloned.1.call-update) | async-done | bytes 4194320 | tf_op jit(solution)/shard_map/psum | solution.py:201
  1017.6 24.3 %all-reduce.7 = (bf16[2048]{0:T(1024)(128)(2,1)S(1)}, bf16[2048]{0:T(1024)(128)(2,1)S(1)}, bf16[2048]{0:T(1024)(128)(2,1)S(1)}, bf16[2048]{0:T(1024)(128)(2,1)S(...) all-reduce(bf16[2048]{0:T(1024)(128)(2,1)S(1)} %add_convert_fusion., ...), channel_id=2, replica_groups=mesh['dp'=8,'mp'=4] {'dp'}, use_global_device_ids=true, to_apply=%region_32.33.clone | all-reduce | flops 12288 | bytes 49152
  1062.7 18.8 %reduce-scatter.9.cloned.1.call-done = bf16[256,2048]{1,0:T(8,128)(2,1)} async-done(((bf16[2048,2048]{1,0:T(8,128)(2,1)}), bf16[256,2048]{1,0:T(8,128)(2,1)}) %reduce-scatter.9.cloned.1.call-update) | async-done | bytes 1048592 | tf_op jit(solution)/shard_map/reduce_scatter | solution.py:215
  1084.3 72.0 %reduce-scatter.11.cloned.1.call-done = bf16[2048,256]{1,0:T(8,128)(2,1)} async-done(((bf16[2048,2048]{1,0:T(8,128)(2,1)}), bf16[2048,256]{1,0:T(8,128)(2,1)}) %reduce-scatter.11.cloned.1.call-update) | async-done | bytes 1048592 | tf_op jit(solution)/shard_map/reduce_scatter | solution.py:218
  1159.0 62.2 %reduce-scatter.5.cloned.1.call-done = bf16[256,3,512]{2,0,1:T(8,128)(2,1)} async-done(((bf16[2048,3,512]{2,0,1:T(8,128)(2,1)}), bf16[256,3,512]{2,0,1:T(8,128)(2,1)}) %reduce-scatter.5.cloned.1.call-update) | async-done | bytes 786448 | tf_op jit(solution)/shard_map/reduce_scatter | solution.py:209
  (414 shorter events, 288.6 us)
Async XLA Ops:
  7.2 52.6 %all-gather.11.cloned.1.call-start = ((), (), s32[]{:S(2)}) async-start(), calls=%async_computation.4 | async-start | bytes 7077888 | tf_op jit(solution)/shard_map/all_gather | solution.py:64
  9.6 80.3 %all-gather.13.cloned.1.call-start = ((), (), s32[]{:S(2)}) async-start(), calls=%async_computation.5 | async-start | bytes 2359296 | tf_op jit(solution)/shard_map/all_gather | solution.py:65
  10.3 170.0 %all-reduce.15.cloned.1.call-start = ((), (), s32[]{:S(2)}) async-start(), calls=%async_computation.6 | async-start | bytes 4194304 | tf_op jit(solution)/shard_map/psum | solution.py:118
  17.4 753.8 %copy-start.97 = (pred[512]{0:T(512)(128)(4,1)}, pred[512]{0:T(512)(128)(4,1)S(1)}, u32[]{:S(2)}) copy-start(pred[512]{0:T(512)(128)(4,1)S(1)} %iota_compare_fusion.2) | copy-start | bytes 1540
  28.1 156.6 %copy-start.56 = (f32[8,1,256]{2,1,0:T(1,128)}, f32[8,1,256]{2,1,0:T(1,128)S(1)}, u32[]{:S(2)}) copy-start(f32[8,1,256]{2,1,0:T(1,128)S(1)} %convert_element_type.455) | copy-start | bytes 24580
  37.0 147.7 %copy-start.93 = (f32[8,1,256]{2,1,0:T(1,128)}, f32[8,1,256]{2,1,0:T(1,128)S(1)}, u32[]{:S(2)}) copy-start(f32[8,1,256]{2,1,0:T(1,128)S(1)} %convert_element_type.456) | copy-start | bytes 24580
  37.1 154.4 %copy-start.64 = (f32[8,64]{1,0:T(8,128)}, f32[8,64]{1,0:T(8,128)S(1)}, u32[]{:S(2)}) copy-start(f32[8,64]{1,0:T(8,128)S(1)} %add.314) | copy-start | bytes 6148
  37.2 157.8 %copy-start.58 = (f32[8,64]{1,0:T(8,128)}, f32[8,64]{1,0:T(8,128)S(1)}, u32[]{:S(2)}) copy-start(f32[8,64]{1,0:T(8,128)S(1)} %add.311) | copy-start | bytes 6148
  73.6 111.1 %copy-start.39 = (bf16[8,64,512]{2,1,0:T(8,128)(2,1)}, bf16[8,64,512]{2,1,0:T(8,128)(2,1)S(1)}, u32[]{:S(2)}) copy-start(bf16[8,64,512]{2,1,0:T(8,128)(2,1)S(1)} %convolution_convert_fusion.11) | copy-start | bytes 1572868
  94.0 193.1 %all-reduce.17.cloned.1.call-start = ((), (), s32[]{:S(2)}) async-start(), calls=%async_computation.9 | async-start | bytes 4194304 | tf_op jit(solution)/shard_map/psum | solution.py:118
  104.1 646.3 %copy-start.99 = (pred[512]{0:T(512)(128)(4,1)}, pred[512]{0:T(512)(128)(4,1)S(1)}, u32[]{:S(2)}) copy-start(pred[512]{0:T(512)(128)(4,1)S(1)} %iota_compare_fusion.1) | copy-start | bytes 1540
  104.2 87.1 %copy-start.60 = (f32[512]{0:T(512)}, f32[512]{0:T(512)S(1)}, u32[]{:S(2)}) copy-start(f32[512]{0:T(512)S(1)} %broadcast_multiply_fusion.2) | copy-start | bytes 6148
  199.2 88.0 %copy-start.10 = (bf16[512,2048]{1,0:T(8,128)(2,1)S(1)}, bf16[512,2048]{1,0:T(8,128)(2,1)}, u32[]{:S(2)}) copy-start(bf16[512,2048]{1,0:T(8,128)(2,1)} %all-reduce.15.cloned.1.call-done) | copy-start | bytes 6291460
  201.8 140.4 %all-gather.15.cloned.1.call-start = ((), (), s32[]{:S(2)}) async-start(), calls=%async_computation.7 | async-start | bytes 9437184 | tf_op jit(solution)/shard_map/all_gather | solution.py:71
  202.4 197.4 %all-gather.17.cloned.1.call-start = ((), (), s32[]{:S(2)}) async-start(), calls=%async_computation.8 | async-start | bytes 9437184 | tf_op jit(solution)/shard_map/all_gather | solution.py:72
  203.0 547.5 %all-reduce.21.cloned.1.call-start = ((), (), s32[]{:S(2)}) async-start(), calls=%async_computation.15 | async-start | bytes 16777216 | tf_op jit(solution)/shard_map/psum | solution.py:127
  221.0 129.9 %copy-start.95 = (f32[8,1,256]{2,1,0:T(1,128)}, f32[8,1,256]{2,1,0:T(1,128)S(1)}, u32[]{:S(2)}) copy-start(f32[8,1,256]{2,1,0:T(1,128)S(1)} %convert_element_type.459) | copy-start | bytes 24580
  292.9 498.5 %copy-start.71 = (f32[512]{0:T(512)}, f32[512]{0:T(512)S(1)}, u32[]{:S(2)}) copy-start(f32[512]{0:T(512)S(1)} %fusion.93) | copy-start | bytes 6148
  292.9 478.3 %copy-start.73 = (f32[512]{0:T(512)}, f32[512]{0:T(512)S(1)}, u32[]{:S(2)}) copy-start(f32[512]{0:T(512)S(1)} %fusion.91) | copy-start | bytes 6148
  459.4 504.0 %reduce-scatter.7.cloned.1.call-start = ((), (), s32[]{:S(2)}) async-start(), calls=%async_computation.11 | async-start | bytes 2359296 | tf_op jit(solution)/shard_map/reduce_scatter | solution.py:212
  803.4 204.2 %all-reduce.19.cloned.1.call-start = ((), (), s32[]{:S(2)}) async-start(), calls=%async_computation.14 | async-start | bytes 8388608 | tf_op jit(solution)/shard_map/psum | solution.py:201
  853.4 228.0 %reduce-scatter.9.cloned.1.call-start = ((), (), s32[]{:S(2)}) async-start(), calls=%async_computation.12 | async-start | bytes 9437184 | tf_op jit(solution)/shard_map/reduce_scatter | solution.py:215
  883.5 272.8 %reduce-scatter.11.cloned.1.call-start = ((), (), s32[]{:S(2)}) async-start(), calls=%async_computation.13 | async-start | bytes 9437184 | tf_op jit(solution)/shard_map/reduce_scatter | solution.py:218
  906.1 315.1 %reduce-scatter.5.cloned.1.call-start = ((), (), s32[]{:S(2)}) async-start(), calls=%async_computation.10 | async-start | bytes 7077888 | tf_op jit(solution)/shard_map/reduce_scatter | solution.py:209
  (116 other events, 1016.1 us)
Sparse Core Ops, SparseCore 0:
  10.5 49.2 all-gather.10
  61.7 28.0 all-gather.12
  94.2 86.1 all-reduce.14
  201.9 85.1 all-reduce.16
  288.9 53.2 all-gather.14
  343.9 55.8 all-gather.16
  459.5 290.8 all-reduce.20
  803.5 40.1 reduce-scatter.6
  853.5 154.0 all-reduce.18
  1010.9 70.5 reduce-scatter.8
  1084.9 71.2 reduce-scatter.10
  1159.5 61.6 reduce-scatter.4
where the time goes:
time: 1240 us; the launch traced here: 1230 us
  waiting for transfers between devices  729 us (59%)
  matrix products  242 us (20%)
  other arithmetic  108 us (9%)
  blocking collectives  105 us (8%)
  local copies, waits for them, and re-layouts  26.2 us (2%)
  between operations  18.9 us (2%)
    psum x1, waiting for transfers between devices, local(): lax.psum(feed_part.astype(jnp.bfloat16), 'mp').astype(jnp.float32)  282 us
    psum x2, waiting for transfers between devices, local(): lax.psum(attention_part.astype(jnp.bfloat16), 'mp').astype(jnp.float32)  142 us
    reduce_scatter x1, waiting for transfers between devices, local(): lax.psum_scatter(acc_reduce.astype(jnp.bfloat16), 'dp', scatter_dimension...  72 us
    reduce_scatter x1, waiting for transfers between devices, local(): lax.psum_scatter(acc_triple.astype(jnp.bfloat16), 'dp', scatter_dimension...  62.2 us
    all_gather x1, waiting for transfers between devices, local(): lax.all_gather(expand_weight, 'dp', axis=0, tiled=True)  49.2 us
    psum x1, waiting for transfers between devices, local(): lax.psum(grad_in_part.astype(jnp.bfloat16), 'mp').astype(jnp.float32)  42.5 us
    dot_general x2, matrix products, local(): jnp.dot(norm_mid, expand_full, preferred_element_type=jnp.float32)  35.1 us
    dot_general x2, matrix products, local(): jnp.dot(norm_mid.T, grad_pre, preferred_element_type=jnp.float32)  29.3 us
  transfers between devices with their start and end apart: 12, of which 11 were waited for; matrix products, arithmetic and copies ran while one was open for 18% of the time, Pallas kernels for 0%

commit v1 on v0

--- a/solution.py
+++ b/solution.py
@@ -7,6 +7,27 @@
 HEAD_DIM = 64
 SLOT = 512
 MICRO = 2
+
+
+def collect(x, axis, dim):
+    length, index, rows = (lax.axis_size(axis), lax.axis_index(axis), x.shape[dim])
+    right = [(i, (i + 1) % length) for i in range(length)]
+    behind = [(i, (i - 1) % length) for i in range(length)]
+    out = jnp.zeros((*x.shape[:dim], length * rows, *x.shape[dim + 1 :]), x.dtype)
+    out = lax.dynamic_update_slice_in_dim(out, x, index * rows, axis=dim)
+    from_left = from_right = x
+    half = length // 2
+    for hop in range(1, half + 1):
+        from_left = lax.ppermute(from_left, axis, right)
+        out = lax.dynamic_update_slice_in_dim(
+            out, from_left, (index - hop) % length * rows, axis=dim
+        )
+        if hop < length - half:
+            from_right = lax.ppermute(from_right, axis, behind)
+            out = lax.dynamic_update_slice_in_dim(
+                out, from_right, (index + hop) % length * rows, axis=dim
+            )
+    return out
 
 
 def layer_norm(values, gain_vec, shift_vec):
@@ -68,7 +89,7 @@
     feed_kept = (
         lax.all_gather(middle_gain, "dp", axis=0, tiled=True),
         lax.all_gather(middle_shift, "dp", axis=0, tiled=True),
-        lax.all_gather(expand_weight, "dp", axis=0, tiled=True),
+        collect(expand_weight, "dp", 0),
         lax.all_gather(reduce_weight, "dp", axis=1, tiled=True),
         lax.all_gather(reduce_bias, "dp", axis=0, tiled=True),
     )

time: 1240 us -> 1180 us (0.952)
  waiting for transfers between devices: 729 us -> 625 us
  blocking collectives: 105 us -> 129 us
  local copies, waits for them, and re-layouts: 26.2 us -> 43.8 us
    psum x2, waiting for transfers between devices: 142 us -> 68.5 us  [local(): lax.psum(attention_part.astype(jnp.bfloat16), 'mp').astype(jnp.float32)]
    reduce_scatter x1, waiting for transfers between devices: 18.8 us -> 72.2 us  [local(): lax.psum_scatter(acc_expand.astype(jnp.bfloat16), 'dp', scatter_dimension...]
    reduce_scatter x1, waiting for transfers between devices: 72 us -> 18.7 us  [local(): lax.psum_scatter(acc_reduce.astype(jnp.bfloat16), 'dp', scatter_dimension...]
    all_gather x1 -> x0, waiting for transfers between devices: 49.2 us -> none  [local(): lax.all_gather(expand_weight, 'dp', axis=0, tiled=True)]
    ppermute x0 -> x7, waiting for transfers between devices: none -> 36.1 us  [the longest x3 35 us: collect(): from_right = lax.ppermute(from_right, axis, behind)]
    all_gather x1, waiting for transfers between devices: 20.4 us -> 3.27 us  [local(): lax.all_gather(reduce_weight, 'dp', axis=1, tiled=True)]
    all_gather x1, blocking collectives: 8.9 us -> 25.6 us  [local(): lax.all_gather(middle_gain, 'dp', axis=0, tiled=True)]
    dynamic_update_slice x0 -> x8, local copies, waits for them, and re-layouts: none -> 13.7 us  [the longest x4 6.8 us: collect(): lax.dynamic_update_slice_in_dim(out, from_left, (index - hop) % length *...]
  transfers between devices with their start and end apart: 12 -> 18, of which waited for: 11 -> 12; matrix products, arithmetic and copies ran while one was open for 18% -> 22% of each run, Pallas kernels for 0% -> 0%
where the time goes in v1:
time: 1180 us; the launch traced here: 1170 us
  waiting for transfers between devices  625 us (53%)
  matrix products  243 us (21%)
  blocking collectives  129 us (11%)
  other arithmetic  109 us (9%)
  local copies, waits for them, and re-layouts  43.8 us (4%)
  between operations  18.7 us (2%)
    psum x1, waiting for transfers between devices, local(): lax.psum(feed_part.astype(jnp.bfloat16), 'mp').astype(jnp.float32)  282 us
    reduce_scatter x1, waiting for transfers between devices, local(): lax.psum_scatter(acc_expand.astype(jnp.bfloat16), 'dp', scatter_dimension...  72.2 us
    psum x2, waiting for transfers between devices, local(): lax.psum(attention_part.astype(jnp.bfloat16), 'mp').astype(jnp.float32)  68.5 us
    reduce_scatter x1, waiting for transfers between devices, local(): lax.psum_scatter(acc_triple.astype(jnp.bfloat16), 'dp', scatter_dimension...  62.3 us
    psum x1, waiting for transfers between devices, local(): lax.psum(grad_in_part.astype(jnp.bfloat16), 'mp').astype(jnp.float32)  42.4 us
    dot_general x2, matrix products, local(): jnp.dot(norm_mid, expand_full, preferred_element_type=jnp.float32)  35.3 us
    ppermute x3, waiting for transfers between devices, collect(): from_right = lax.ppermute(from_right, axis, behind)  35 us
    dot_general x2, matrix products, local(): jnp.dot(norm_mid.T, grad_pre, preferred_element_type=jnp.float32)  29.4 us
  transfers between devices with their start and end apart: 18, of which 12 were waited for; matrix products, arithmetic and copies ran while one was open for 22% of the time, Pallas kernels for 0%

profile of v1, /device:TPU:0, one launch (start us, length us, event | category | flops | bytes accessed | tf_op | source)
XLA Modules:
  0.0 1174.5 jit_solution(3290260676207367767)
XLA Ops:
  17.5 10.6 all-gather
  37.4 22.4 %all-gather.10.cloned.1.call-done = bf16[2048,3,512]{0,2,1:T(8,128)(2,1)} async-done(((bf16[256,3,512]{0,2,1:T(8,128)(2,1)}), bf16[2048,3,512]{0,2,1:T(8,128)(2,1)}) %all-gather.10.cloned.1.call-update) | async-done | bytes 6291472 | tf_op jit(solution)/shard_map/all_gather | solution.py:85
  73.6 16.3 %all-gather.12.cloned.1.call-done = bf16[512,2048]{1,0:T(8,128)(2,1)} async-done(((bf16[512,256]{1,0:T(8,128)(2,1)}), bf16[512,2048]{1,0:T(8,128)(2,1)}) %all-gather.12.cloned.1.call-update) | async-done | bytes 2097168 | tf_op jit(solution)/shard_map/all_gather | solution.py:86
  94.4 16.6 %all-gather.2 = bf16[8,1,256]{2,1,0:T(2,128)(2,1)S(1)} all-gather(bf16[1,1,256]{2,1,0:T(2,128)(2,1)S(1)} %reshape.370), channel_id=1, replica_groups=mesh['dp'=8,'mp'=4] {'dp'}, dimensions={0}, use_global_device_ids=true | all-gather | bytes 4608 | tf_op jit(solution)/shard_map/all_gather | solution.py:87
  111.8 68.5 %all-reduce.15.cloned.1.call-done = bf16[512,2048]{1,0:T(8,128)(2,1)} async-done(((bf16[512,2048]{1,0:T(8,128)(2,1)}), bf16[512,2048]{1,0:T(8,128)(2,1)}) %all-reduce.15.cloned.1.call-update) | async-done | bytes 2097168 | tf_op jit(solution)/shard_map/psum | solution.py:139
  202.9 23.1 %collective-permute-done.1 = bf16[256,2048]{1,0:T(8,128)(2,1)} collective-permute-done((bf16[256,2048]{1,0:T(8,128)(2,1)S(1)}, bf16[256,2048]{1,0:T(8,128)(2,1)}, u32[]{:S(2)}, u32[]{:S(2)}) %collective-permute-start.1) | collective-permute-done | bytes 1048608 | tf_op jit(solution)/shard_map/ppermute | solution.py:26
  229.4 25.6 %all-gather.3 = bf16[8,1,256]{2,1,0:T(2,128)(2,1)S(1)} all-gather(bf16[1,1,256]{2,1,0:T(2,128)(2,1)S(1)} %reshape.372), channel_id=1, replica_groups=mesh['dp'=8,'mp'=4] {'dp'}, dimensions={0}, use_global_device_ids=true | all-gather | bytes 4608 | tf_op jit(solution)/shard_map/all_gather | solution.py:90
  281.5 11.9 %collective-permute-done.5 = bf16[256,2048]{1,0:T(8,128)(2,1)S(1)} collective-permute-done((bf16[256,2048]{1,0:T(8,128)(2,1)}, bf16[256,2048]{1,0:T(8,128)(2,1)S(1)}, u32[]{:S(2)}, u32[]{:S(2)}) %collective-permute-start.5) | collective-permute-done | bytes 1048608 | tf_op jit(solution)/shard_map/ppermute | solution.py:26
  312.1 27.9 %multiply_convert_fusion.3 = (bf16[512,2048]{1,0:T(8,128)(2,1)}, f32[512,2048]{1,0:T(8,128)}, bf16[512,2048]{1,0:T(8,128)(2,1)}, f32[512,2048]{1,0:T(8,128)}, f32[512,2048]{1,0:T(8,128)}) fusion(f32[2048]{0:T(1024)S(1)} %convert_element_type.369, f32[512,2048]{1,0:T(8,128)S(1)} %fusion.108, bf16[2048,2048]{1,0:T(8,128)(2,1)} %constant_dynamic-update-slice_fusion, ...), kind=kOutput, calls=%fused_computation.120 | convolution fusion | flops 4442816512 | bytes 33591296 | tf_op jit(solution)/shard_map/dot_general | solution.py:145
  343.3 13.2 %convert_reduce_fusion.6 = (f32[2048]{0:T(1024)}, bf16[512,2048]{1,0:T(8,128)(2,1)S(1)}) fusion(f32[512,2048]{1,0:T(8,128)} %get-tuple-element.85, bf16[2048,2048]{1,0:T(8,128)(2,1)} %all-gather.14.cloned.1.call-done, pred[512]{0:T(512)(128)(4,1)S(1)} %iota_compare_fusion.1, bf16[1024,2048]{1,0:T(8,128)(2,1)} %param.16, f32[512,2048]{1,0:T(8,128)} %copy-done.120, ...), kind=kOutput, calls=%fused_computation.81 | convolution fusion | flops 4315936768 | bytes 20988416 | tf_op jit(solution)/shard_map/dot_general | solution.py:167
  366.4 11.5 convert_reduce_fusion.7
  377.9 9.9 convolution_convert_fusion.1
  412.6 281.5 %all-reduce.21.cloned.1.call-done = (bf16[512,2048]{1,0:T(8,128)(2,1)}, bf16[512,2048]{1,0:T(8,128)(2,1)}, bf16[512,2048]{1,0:T(8,128)(2,1)}, bf16[512,2048]{1,0:T(8,128)(2,1)}) async-done(((bf16[512,2048]{1,0:T(8,128)(2,1)}, bf16[512,2048]{1,0:T(8,128)(2,1)}, bf16[512,2048]{1,0:T(8,128)(2,1)}, bf16[512,2048]{1,0:T(8,128)(2,1)}), (bf16[512,2048]{1,0:T(8,128)(2,1)}, bf16[512,2048]{1,0:T(8,128)(2,1)}, ...) | async-done | bytes 8388624 | tf_op jit(solution)/shard_map/psum | solution.py:148
  694.2 14.7 %select_reduce_fusion.5 = (f32[]{:T(128)}, f32[512]{0:T(512)S(1)}, f32[512]{0:T(512)S(1)}, f32[]{:T(128)}, f32[]{:T(128)}, /*index=5*/f32[]{:T(128)}, f32[]{:T(1...) fusion(bf16[512,2048]{1,0:T(8,128)(2,1)} %get-tuple-element.67,, ...), kind=kLoop, calls=%fused_computation.80 | loop fusion | flops 55567360 | bytes 25224216 | tf_op jit(solution)/shard_map/reduce_sum | solution.py:155
  798.8 10.2 fusion.71
  809.0 11.0 add_convert_fusion
  820.7 13.9 %fusion.106 = f32[2048,2048]{1,0:T(8,128)} fusion(bf16[512,2048]{1,0:T(8,128)(2,1)} %copy-done.119, f32[2048]{0:T(1024)S(1)} %bitcast.180, f32[2048]{0:T(1024)S(1)} %bitcast.161, f32[512]{0:T(512)S(1)} %copy-done.74, bf16[512,2048]{1,0:T(8,128)(2,1)} %all-reduce.15.cloned.1.call-done, f32[512]{0:T(512)S(1)} %broadcast_multiply_fusion.3, ...), kind=kOutput, calls=%fused_computation.257 | convolution fusion | flops 4304404480 | bytes 23097344 | tf_op jit(solution)/shard_map/dot_general | solution.py:171
  834.5 15.5 %add_convert_fusion.1 = bf16[2048,2048]{1,0:T(8,128)(2,1)} fusion(f32[2048,2048]{1,0:T(8,128)} %fusion.106, bf16[512,2048]{1,0:T(8,128)(2,1)} %copy-done.121, f32[512]{0:T(512)S(1)} %copy-done.72, f32[2048]{0:T(1024)S(1)} %bitcast.181, f32[2048]{0:T(1024)S(1)} %bitcast.162, bf16[512,2048]{1,0:T(8,128)(2,1)} %all-reduce.17.cloned.1.call-done, ...), kind=kOutput, calls=%fused_computation.1 | convolution fusion | flops 4312793088 | bytes 31485952 | tf_op jit(solution)/shard_map/dot_general | solution.py:171
  875.9 25.3 %all-reduce.6 = (f32[2,512]{1,0:T(2,128)}, f32[2048]{0:T(1024)}, f32[4]{0:T(128)S(1)}) all-reduce(f32[2,512]{1,0:T(2,128)S(1)} %maximum_add_fusion, f32[2048]{0:T(1024)S(1)} %add.437, f32[4]{0:T(128)S(1)} %maximum_add_fusion.1), channel_id=1, replica_groups=mesh['dp'=8,'mp'=4] {'dp'}, use_global_device_ids=true, to_apply=%region_41.42 | all-reduce | flops 3076 | bytes 24608 | tf_op jit(solution)/shard_map/psum | solution.py:261
  908.9 42.4 %all-reduce.19.cloned.1.call-done = (bf16[512,2048]{1,0:T(8,128)(2,1)}, bf16[512,2048]{1,0:T(8,128)(2,1)}) async-done(((bf16[512,2048]{1,0:T(8,128)(2,1)}, bf16[512,2048]{1,0:T(8,128)(2,1)}), (bf16[512,2048]{1,0:T(8,128)(2,1)}, bf16[512,2048]{1,0:T(8,128)(2,1)})) %all-reduce.19.cloned.1.call-update) | async-done | bytes 4194320 | tf_op jit(solution)/shard_map/psum | solution.py:222
  961.4 24.3 %all-reduce.7 = (bf16[2048]{0:T(1024)(128)(2,1)S(1)}, bf16[2048]{0:T(1024)(128)(2,1)S(1)}, bf16[2048]{0:T(1024)(128)(2,1)S(1)}, bf16[2048]{0:T(1024)(128)(2,1)S(...) all-reduce(bf16[2048]{0:T(1024)(128)(2,1)S(1)} %add_convert_fusion., ...), channel_id=2, replica_groups=mesh['dp'=8,'mp'=4] {'dp'}, use_global_device_ids=true, to_apply=%region_32.33.clone | all-reduce | flops 12288 | bytes 49152
  1006.5 18.7 %reduce-scatter.11.cloned.1.call-done = bf16[2048,256]{1,0:T(8,128)(2,1)} async-done(((bf16[2048,2048]{1,0:T(8,128)(2,1)}), bf16[2048,256]{1,0:T(8,128)(2,1)}) %reduce-scatter.11.cloned.1.call-update) | async-done | bytes 1048592 | tf_op jit(solution)/shard_map/reduce_scatter | solution.py:239
  1027.9 72.2 %reduce-scatter.9.cloned.1.call-done = bf16[256,2048]{1,0:T(8,128)(2,1)} async-done(((bf16[2048,2048]{1,0:T(8,128)(2,1)}), bf16[256,2048]{1,0:T(8,128)(2,1)}) %reduce-scatter.9.cloned.1.call-update) | async-done | bytes 1048592 | tf_op jit(solution)/shard_map/reduce_scatter | solution.py:236
  1102.9 62.3 %reduce-scatter.5.cloned.1.call-done = bf16[256,3,512]{2,0,1:T(8,128)(2,1)} async-done(((bf16[2048,3,512]{2,0,1:T(8,128)(2,1)}), bf16[256,3,512]{2,0,1:T(8,128)(2,1)}) %reduce-scatter.5.cloned.1.call-update) | async-done | bytes 786448 | tf_op jit(solution)/shard_map/reduce_scatter | solution.py:230
  (434 shorter events, 306.3 us)
Async XLA Ops:
  7.2 52.6 %all-gather.10.cloned.1.call-start = ((), (), s32[]{:S(2)}) async-start(), calls=%async_computation.4 | async-start | bytes 7077888 | tf_op jit(solution)/shard_map/all_gather | solution.py:85
  9.6 80.3 %all-gather.12.cloned.1.call-start = ((), (), s32[]{:S(2)}) async-start(), calls=%async_computation.5 | async-start | bytes 2359296 | tf_op jit(solution)/shard_map/all_gather | solution.py:86
  10.3 170.0 %all-reduce.15.cloned.1.call-start = ((), (), s32[]{:S(2)}) async-start(), calls=%async_computation.6 | async-start | bytes 4194304 | tf_op jit(solution)/shard_map/psum | solution.py:139
  28.1 156.6 %copy-start.56 = (f32[8,1,256]{2,1,0:T(1,128)}, f32[8,1,256]{2,1,0:T(1,128)S(1)}, u32[]{:S(2)}) copy-start(f32[8,1,256]{2,1,0:T(1,128)S(1)} %convert_element_type.455) | copy-start | bytes 24580
  37.1 153.9 %copy-start.64 = (f32[8,64]{1,0:T(8,128)}, f32[8,64]{1,0:T(8,128)S(1)}, u32[]{:S(2)}) copy-start(f32[8,64]{1,0:T(8,128)S(1)} %add.373) | copy-start | bytes 6148
  37.2 157.2 %copy-start.58 = (f32[8,64]{1,0:T(8,128)}, f32[8,64]{1,0:T(8,128)S(1)}, u32[]{:S(2)}) copy-start(f32[8,64]{1,0:T(8,128)S(1)} %add.370) | copy-start | bytes 6148
  94.0 202.6 %all-reduce.17.cloned.1.call-start = ((), (), s32[]{:S(2)}) async-start(), calls=%async_computation.8 | async-start | bytes 4194304 | tf_op jit(solution)/shard_map/psum | solution.py:139
  94.1 108.8 %collective-permute-start = (bf16[256,2048]{1,0:T(8,128)(2,1)S(1)}, bf16[256,2048]{1,0:T(8,128)(2,1)S(1)}, u32[]{:S(2)}, u32[]{:S(2)}) collective-permute-start(bf16[256,2048]{1,0:T(8,128)(2,1)S(1)} %copy-done.40), channel_id=1, source_target_pairs={{0,4},{4,8},{8,12},{12,16},{16,20},{20,24},{24,28},{28,0},{1,5},{5... | collective-permute-start | bytes 3145736 | tf_op jit(solution)/shard_map/ppermute | solution.py:21
  111.6 582.5 %copy-start.100 = (pred[512]{0:T(512)(128)(4,1)}, pred[512]{0:T(512)(128)(4,1)S(1)}, u32[]{:S(2)}) copy-start(pred[512]{0:T(512)(128)(4,1)S(1)} %iota_compare_fusion.1) | copy-start | bytes 1540
  201.3 142.0 %all-gather.14.cloned.1.call-start = ((), (), s32[]{:S(2)}) async-start(), calls=%async_computation.7 | async-start | bytes 9437184 | tf_op jit(solution)/shard_map/all_gather | solution.py:93
  201.3 24.6 %collective-permute-start.1 = (bf16[256,2048]{1,0:T(8,128)(2,1)S(1)}, bf16[256,2048]{1,0:T(8,128)(2,1)}, u32[]{:S(2)}, u32[]{:S(2)}) collective-permute-start(bf16[256,2048]{1,0:T(8,128)(2,1)S(1)} %copy-done.40), channel_id=1, source_target_pairs={{0,28},{4,0},{8,4},{12,8},{16,12},{20,16},{24,20},{28,24},{1,29},{... | collective-permute-start | bytes 3145736 | tf_op jit(solution)/shard_map/ppermute | solution.py:26
  202.9 26.3 %collective-permute-start.2 = (bf16[256,2048]{1,0:T(8,128)(2,1)S(1)}, bf16[256,2048]{1,0:T(8,128)(2,1)}, u32[]{:S(2)}, u32[]{:S(2)}) collective-permute-start(bf16[256,2048]{1,0:T(8,128)(2,1)S(1)} %collective-permute-done), channel_id=1, source_target_pairs={{0,4},{4,8},{8,12},{12,16},{16,20},{20,24},{24,28},{28,0},{1,5},{5... | collective-permute-start | bytes 3145736 | tf_op jit(solution)/shard_map/ppermute | solution.py:21
  225.9 43.5 %collective-permute-start.3 = (bf16[256,2048]{1,0:T(8,128)(2,1)}, bf16[256,2048]{1,0:T(8,128)(2,1)}, u32[]{:S(2)}, u32[]{:S(2)}) collective-permute-start(bf16[256,2048]{1,0:T(8,128)(2,1)} %collective-permute-done.1), channel_id=1, source_target_pairs={{0,28},{4,0},{8,4},{12,8},{16,12},{20,16},{24,20},{28,24},{1,29},{... | collective-permute-start | bytes 3145736 | tf_op jit(solution)/shard_map/ppermute | solution.py:26
  229.1 42.7 %collective-permute-start.4 = (bf16[256,2048]{1,0:T(8,128)(2,1)}, bf16[256,2048]{1,0:T(8,128)(2,1)}, u32[]{:S(2)}, u32[]{:S(2)}) collective-permute-start(bf16[256,2048]{1,0:T(8,128)(2,1)} %collective-permute-done.2), channel_id=1, source_target_pairs={{0,4},{4,8},{8,12},{12,16},{16,20},{20,24},{24,28},{28,0},{1,5},{5... | collective-permute-start | bytes 3145736 | tf_op jit(solution)/shard_map/ppermute | solution.py:21
  229.2 465.0 %all-reduce.21.cloned.1.call-start = ((), (), s32[]{:S(2)}) async-start(), calls=%async_computation.14 | async-start | bytes 16777216 | tf_op jit(solution)/shard_map/psum | solution.py:148
  269.5 23.9 %collective-permute-start.5 = (bf16[256,2048]{1,0:T(8,128)(2,1)}, bf16[256,2048]{1,0:T(8,128)(2,1)S(1)}, u32[]{:S(2)}, u32[]{:S(2)}) collective-permute-start(bf16[256,2048]{1,0:T(8,128)(2,1)} %collective-permute-done.3), channel_id=1, source_target_pairs={{0,28},{4,0},{8,4},{12,8},{16,12},{20,16},{24,20},{28,24},{1,29},{... | collective-permute-start | bytes 3145736 | tf_op jit(solution)/shard_map/ppermute | solution.py:26
  271.8 23.7 %collective-permute-start.6 = (bf16[256,2048]{1,0:T(8,128)(2,1)}, bf16[256,2048]{1,0:T(8,128)(2,1)S(1)}, u32[]{:S(2)}, u32[]{:S(2)}) collective-permute-start(bf16[256,2048]{1,0:T(8,128)(2,1)} %collective-permute-done.4), channel_id=1, source_target_pairs={{0,4},{4,8},{8,12},{12,16},{16,20},{20,24},{24,28},{28,0},{1,5},{5... | collective-permute-start | bytes 3145736 | tf_op jit(solution)/shard_map/ppermute | solution.py:21
  302.6 432.6 %copy-start.71 = (f32[512]{0:T(512)}, f32[512]{0:T(512)S(1)}, u32[]{:S(2)}) copy-start(f32[512]{0:T(512)S(1)} %fusion.93) | copy-start | bytes 6148
  302.7 412.3 %copy-start.73 = (f32[512]{0:T(512)}, f32[512]{0:T(512)S(1)}, u32[]{:S(2)}) copy-start(f32[512]{0:T(512)S(1)} %fusion.91) | copy-start | bytes 6148
  403.1 504.1 %reduce-scatter.7.cloned.1.call-start = ((), (), s32[]{:S(2)}) async-start(), calls=%async_computation.10 | async-start | bytes 2359296 | tf_op jit(solution)/shard_map/reduce_scatter | solution.py:233
  747.2 204.2 %all-reduce.19.cloned.1.call-start = ((), (), s32[]{:S(2)}) async-start(), calls=%async_computation.13 | async-start | bytes 8388608 | tf_op jit(solution)/shard_map/psum | solution.py:222
  797.2 228.0 %reduce-scatter.11.cloned.1.call-start = ((), (), s32[]{:S(2)}) async-start(), calls=%async_computation.12 | async-start | bytes 9437184 | tf_op jit(solution)/shard_map/reduce_scatter | solution.py:239
  820.0 280.1 %reduce-scatter.9.cloned.1.call-start = ((), (), s32[]{:S(2)}) async-start(), calls=%async_computation.11 | async-start | bytes 9437184 | tf_op jit(solution)/shard_map/reduce_scatter | solution.py:236
  850.1 315.0 %reduce-scatter.5.cloned.1.call-start = ((), (), s32[]{:S(2)}) async-start(), calls=%async_computation.9 | async-start | bytes 7077888 | tf_op jit(solution)/shard_map/reduce_scatter | solution.py:230
  (122 other events, 1596.0 us)
Sparse Core Ops, SparseCore 0:
  10.5 49.2 all-gather.9
  61.7 28.0 all-gather.11
  94.2 86.1 all-reduce.14
  201.4 85.1 all-reduce.16
  288.3 54.8 all-gather.13
  403.2 290.8 all-reduce.20
  747.3 40.0 reduce-scatter.6
  797.3 153.9 all-reduce.18
  954.9 70.3 reduce-scatter.10
  1028.5 71.5 reduce-scatter.8
  1103.4 61.6 reduce-scatter.4
